TPU v7x, 32 devices: a whole 2x2x4 slice. The times are simulated.
32 devices in a mesh: img: 4 (over x, core), patch: 8 (over z, y).
Axes of the slice: x: 2, y: 2, z: 4, core: 2. Of those that a mesh axis runs over, the one named last changes fastest.
Arguments:
- hidden: bfloat16 [8, 8, 128, 640], P('img', 'patch'), may hold values from -100 to 100
- stale_attn_in: bfloat16 [8, 8, 128, 640], P('img', 'patch'), may hold values from -100 to 100
- stale_conv_in: bfloat16 [8, 8, 128, 640], P('img', 'patch'), may hold values from -6 to 6
- ln_gain: float32 [640], replicated, may hold values from 0.25 to 1.75
- ln_bias: float32 [640], replicated, may hold values from -2 to 2
- w_qkv: bfloat16 [640, 1920], replicated, may hold values from -3 to 3
- w_out: bfloat16 [640, 640], replicated, may hold values from -0.25 to 0.25
- gn_gain: float32 [640], replicated, may hold values from 0.25 to 1.75
- gn_bias: float32 [640], replicated, may hold values from -1.5 to 1.5
- conv_weight: bfloat16 [3, 3, 640, 640], replicated, may hold values from -0.078125 to 0.078125
- conv_bias: float32 [640], replicated, may hold values from -1.5 to 1.5
- time_shift: float32 [8, 640], P('img'), may hold values from -6 to 6
Outputs:
- block_out: bfloat16 [8, 8, 128, 640], P('img', 'patch')
All inputs are finite; a program needn't handle non-finite values.
Results may differ from a plain program's by a relative error of at most 0.0075.
The roundings to bfloat16 on the way count: a program that leaves them out, or rounds other values in their place, can miss the bound.
Values may be sent and summed in bfloat16 or wider, within the bound.
A program may use at most 128 MiB of HBM per device.

v0:
```python
import jax
import jax.numpy as jnp
from jax import lax
from jax.sharding import PartitionSpec as P

GROUPS = 32
HEAD_DIM = 64
EPSILON = 1e-05


def extended(block, sides, width):
    for axis, dim in sides:
        count = lax.axis_size(axis)
        forward = [(i, i + 1) for i in range(count - 1)]
        backward = [(target, source) for source, target in forward]
        low = lax.ppermute(
            lax.slice_in_dim(block, block.shape[dim] - width, None, axis=dim), axis, forward
        )
        high = lax.ppermute(lax.slice_in_dim(block, 0, width, axis=dim), axis, backward)
        block = jnp.concatenate([low, block, high], axis=dim)
    return block


def layer_norm(values, gain, bias):
    values = values.astype(jnp.float32)
    centre = jnp.mean(values, -1, keepdims=True)
    centred = values - centre
    spread = jnp.mean(centred * centred, -1, keepdims=True)
    return (centred * lax.rsqrt(spread + EPSILON) * gain + bias).astype(jnp.bfloat16)


def absorb(softmax_state, queries, key_rows, value_rows, blocked):
    running_max, weight_sum, accum = softmax_state
    samples, key_count, channels = key_rows.shape
    head_count = channels // HEAD_DIM
    keys_split = key_rows.reshape(samples, key_count, head_count, HEAD_DIM)
    values_split = value_rows.reshape(samples, key_count, head_count, HEAD_DIM)
    scores = jnp.einsum(
        "sqhd,skhd->shqk", queries, keys_split, preferred_element_type=jnp.float32
    ) * HEAD_DIM ** (-0.5)
    scores = jnp.where(blocked[None, None, None, :], -jnp.inf, scores)
    new_max = jnp.maximum(running_max, jnp.max(scores, -1))
    rescale = jnp.exp(running_max - new_max)
    weights = jnp.exp(scores - new_max[..., None])
    weight_sum = weight_sum * rescale + jnp.sum(weights, -1)
    accum = accum * rescale[..., None] + jnp.einsum(
        "shqk,skhd->shqd",
        weights.astype(jnp.bfloat16),
        values_split,
        preferred_element_type=jnp.float32,
    )
    return (new_max, weight_sum, accum)


def shards(
    hidden,
    stale_attn_in,
    stale_conv_in,
    ln_gain,
    ln_bias,
    w_qkv,
    w_out,
    gn_gain,
    gn_bias,
    conv_weight,
    conv_bias,
    time_shift,
):
    samples, rows_dev, col_count, channels = hidden.shape
    head_count = channels // HEAD_DIM
    local_count = rows_dev * col_count
    own_start = lax.axis_index("patch") * local_count
    fresh_in = layer_norm(hidden, ln_gain, ln_bias).reshape(samples, local_count, channels)
    stale_in = layer_norm(stale_attn_in, ln_gain, ln_bias).reshape(samples, local_count, channels)
    fresh_qkv = jnp.einsum(
        "stc,cd->std", fresh_in, w_qkv, preferred_element_type=jnp.float32
    ).astype(jnp.bfloat16)
    queries = fresh_qkv[..., :channels].reshape(samples, local_count, head_count, HEAD_DIM)
    w_pair = w_qkv[:, channels:]
    initial = (
        jnp.full((samples, head_count, local_count), -jnp.inf, jnp.float32),
        jnp.zeros((samples, head_count, local_count), jnp.float32),
        jnp.zeros((samples, head_count, local_count, HEAD_DIM), jnp.float32),
    )
    no_block = jnp.zeros((local_count,), bool)
    softmax_state = absorb(
        initial,
        queries,
        fresh_qkv[..., channels : 2 * channels],
        fresh_qkv[..., 2 * channels :],
        no_block,
    )
    block_rows = lax.all_gather(stale_in, "patch", axis=1, tiled=True)
    pair_rows = jnp.einsum(
        "snc,cd->snd", block_rows, w_pair, preferred_element_type=jnp.float32
    ).astype(jnp.bfloat16)
    positions = jnp.arange(block_rows.shape[1], dtype=jnp.int32)
    blocked = (positions >= own_start) & (positions < own_start + local_count)
    softmax_state = absorb(
        softmax_state, queries, pair_rows[..., :channels], pair_rows[..., channels:], blocked
    )
    running_max, weight_sum, accum = softmax_state
    attended = (
        (accum / weight_sum[..., None])
        .transpose(0, 2, 1, 3)
        .reshape(samples, local_count, channels)
        .astype(jnp.bfloat16)
    )
    attention_out = jnp.einsum("stc,cd->std", attended, w_out, preferred_element_type=jnp.float32)
    residual = (
        hidden.reshape(samples, local_count, channels).astype(jnp.float32) + attention_out
    ).astype(jnp.bfloat16)
    grouped = residual.astype(jnp.float32).reshape(samples, local_count, GROUPS, channels // GROUPS)
    cell_count = lax.axis_size("patch") * local_count * (channels // GROUPS)
    group_mean = lax.psum(jnp.sum(grouped, axis=(1, 3)), "patch") / cell_count
    centred = grouped - group_mean[:, None, :, None]
    group_var = lax.psum(jnp.sum(centred * centred, axis=(1, 3)), "patch") / cell_count
    normalized = (centred * lax.rsqrt(group_var + EPSILON)[:, None, :, None]).reshape(
        samples, local_count, channels
    )
    activated = (
        jax.nn.silu(normalized * gn_gain + gn_bias)
        .astype(jnp.bfloat16)
        .reshape(samples, rows_dev, col_count, channels)
    )
    stale_framed = extended(stale_conv_in, (("patch", 1),), 1)
    framed = jnp.concatenate([stale_framed[:, :1], activated, stale_framed[:, rows_dev + 1 :]], 1)
    framed = jnp.pad(framed, ((0, 0), (0, 0), (1, 1), (0, 0)))
    windows = [
        framed[:, tap_row : tap_row + rows_dev, tap_col : tap_col + col_count, :]
        for tap_row in range(3)
        for tap_col in range(3)
    ]
    unfolded = jnp.concatenate(windows, -1).reshape(samples * local_count, 9 * channels)
    convolved = jnp.dot(
        unfolded, conv_weight.reshape(9 * channels, channels), preferred_element_type=jnp.float32
    )
    summed_out = (
        convolved.reshape(samples, rows_dev, col_count, channels)
        + conv_bias
        + time_shift[:, None, None, :]
        + residual.astype(jnp.float32).reshape(samples, rows_dev, col_count, channels)
    )
    return summed_out.astype(jnp.bfloat16)


def solution(mesh):
    in_specs = (
        P("img", "patch", None, None),
        P("img", "patch", None, None),
        P("img", "patch", None, None),
        P(),
        P(),
        P(),
        P(),
        P(),
        P(),
        P(),
        P(),
        P("img", None),
    )
    out_specs = P("img", "patch", None, None)
    return jax.shard_map(shards, mesh=mesh, in_specs=in_specs, out_specs=out_specs, check_vma=False)
```

profile of v0, /device:TPU:0, one launch (start us, length us, event | category | flops | bytes accessed | tf_op | source)
XLA Modules:
  0.0 154.2 jit_solution(17788992651743523699)
XLA Ops:
  6.5 1.2 convert_reduce_fusion.1
  7.7 1.2 fusion.54
  8.9 1.9 %fusion.57 = bf16[2,1,128,640]{3,2,0,1:T(8,128)(2,1)} fusion(bf16[2,1,128,640]{3,2,1,0:T(8,128)(2,1)} %param.13, f32[2,128]{1,0:T(2,128)S(1)} %add_rsqrt_fusion.1, f32[2,128]{1,0:T(2,128)S(1)} %broadcast_multiply_fusion.1, f32[640]{0:T(1024)} %param.16, f32[640]{0:T(1024)} %param.15), kind=kLoop, calls=%fused_computation.59 | loop fusion | flops 983040 | bytes 662528 | tf_op jit(solution)/shard_map/convert_element_type | solution.py:29
  10.9 1.3 collective-permute-start.1
  12.2 6.3 %collective-permute-start = (bf16[2,1,128,640]{3,2,0,1:T(8,128)(2,1)}, bf16[2,1,128,640]{3,2,0,1:T(8,128)(2,1)}, u32[]{:S(2)}, u32[]{:S(2)}) collective-permute-start(bf16[2,1,128,640]{3,2,0,1:T(8,128)(2,1)} %bitcast.117), channel_id=1, source_target_pairs={{0,1},{1,2},{2,3},{3,4},{4,5},{5,6},{6,7},{8,9},{9,10},{10,11},{11... | collective-permute-start | bytes 983048 | tf_op jit(solution)/shard_map/ppermute | solution.py:16
  18.5 1.1 convert_reduce_fusion
  19.6 1.2 fusion.50
  20.8 3.0 %convolution_convert_fusion.1 = bf16[2,128,1920]{2,1,0:T(8,128)(2,1)S(1)} fusion(bf16[640,1920]{1,0:T(8,128)(2,1)} %param.17, bf16[2,1,128,640]{3,2,1,0:T(8,128)(2,1)} %param.12, f32[640]{0:T(1024)} %param.16, f32[640]{0:T(1024)} %param.15, f32[2,128]{1,0:T(2,128)S(1)} %add_rsqrt_fusion.2, f32[2,128]{1,0:T(2,128)S(1)} %broadcast_multiply_fusion.2), kind=kOutput, calls=%fused_computation.13 | convolution fusion | flops 630620160 | bytes 3775488 | tf_op jit(solution)/shard_map/stc,cd->std/dot_general | solution.py:75
  24.4 0.9 copy.30
  25.7 1.1 copy-done.1
  27.0 46.8 %all-gather.3.cloned.1.call-done = bf16[2,1,1024,640]{3,2,0,1:T(8,128)(2,1)} async-done(((bf16[2,1,128,640]{3,2,0,1:T(8,128)(2,1)}), bf16[2,1,1024,640]{3,2,0,1:T(8,128)(2,1)}) %all-gather.3.cloned.1.call-update) | async-done | bytes 2621456 | tf_op jit(solution)/shard_map/all_gather | solution.py:93
  73.9 6.5 %convolution_convert_fusion = bf16[2,1024,1280]{2,1,0:T(8,128)(2,1)S(1)} fusion(bf16[2,1,1024,640]{3,2,0,1:T(8,128)(2,1)} %all-gather.3.cloned.1.call-done, bf16[640,1920]{1,0:T(8,128)(2,1)} %param.17), kind=kOutput, calls=%fused_computation.5 | convolution fusion | flops 3358064640 | bytes 9502720 | tf_op jit(solution)/shard_map/snc,cd->snd/dot_general | solution.py:94
  80.3 2.0 %fusion.76 = (bf16[2,1024,640]{2,1,0:T(8,128)(2,1)S(1)}, bf16[2,1024,640]{2,1,0:T(8,128)(2,1)}) fusion(bf16[2,1024,1280]{2,1,0:T(8,128)(2,1)S(1)} %convolution_convert_fusion), kind=kLoop, calls=%fused_computation.98 | loop fusion | bytes 10485760 | tf_op jit(solution)/shard_map/slice | solution.py:100
  82.3 4.5 %copy.34 = bf16[2,1024,640]{1,2,0:T(8,128)(2,1)} copy(bf16[2,1024,640]{2,1,0:T(8,128)(2,1)} %get-tuple-element.8) | data formatting | bytes 5242880 | tf_op jit(solution)/shard_map/slice | solution.py:100
  86.9 2.7 %copy.33 = bf16[2,1024,640]{1,2,0:T(8,128)(2,1)} copy(bf16[2,1024,640]{2,1,0:T(8,128)(2,1)S(1)} %get-tuple-element.7) | data formatting | bytes 5242880 | tf_op jit(solution)/shard_map/slice | solution.py:100
  89.6 3.5 %fusion = (f32[2,10,128]{2,1,0:T(8,128)S(1)}, f32[2,10,128,1024]{3,2,1,0:T(8,128)S(1)}) fusion(pred[1024]{0:T(1024)(128)(4,1)S(1)} %fusion.72, bf16[2,128,10,64]{1,3,2,0:T(8,128)(2,1)} %bitcast.110, bf16[2,1024,10,64]{1,3,2,0:T(8,128)(2,1)} %bitcast.108), kind=kOutput, calls=%fused_computation.2 | convolution fusion | flops 343406080 | bytes 13446144 | tf_op jit(solution)/shard_map/sqhd,skhd->shqk/dot_general | solution.py:38
  93.1 2.5 %fusion.1 = f32[2,10,128]{2,1,0:T(8,128)S(1)} fusion(f32[2,10,128,1024]{3,2,1,0:T(8,128)S(1)} %get-tuple-element.16, f32[2,10,128]{2,1,0:T(8,128)S(1)} %max.18, pred[1024]{0:T(1024)(128)(4,1)S(1)} %fusion.72), kind=kLoop, calls=%fused_computation.3 | loop fusion | flops 10483200 | bytes 10507264 | tf_op jit(solution)/shard_map/reduce_sum | solution.py:45
  95.6 2.4 %fusion.13 = f32[2,128,10,64]{1,3,2,0:T(8,128)S(1)} fusion(bf16[2,1024,10,64]{1,3,2,0:T(8,128)(2,1)S(1)} %bitcast.111, f32[2,10,128,1024]{3,2,1,0:T(8,128)S(1)} %get-tuple-element.16, f32[2,10,128]{2,1,0:T(8,128)S(1)} %max.18, pred[1024]{0:T(1024)(128)(4,1)S(1)} %fusion.72), kind=kOutput, calls=%fused_computation.20 | convolution fusion | flops 346030080 | bytes 13773824 | tf_op jit(solution)/shard_map/shqk,skhd->shqd/dot_general | solution.py:46
  99.7 19.0 %psum.14 = f32[2,32]{1,0:T(2,128)S(1)} all-reduce(f32[2,32]{1,0:T(2,128)S(1)} %reduce_sum.100), channel_id=1, replica_groups=mesh['img'=4,'patch'=8] {'patch'}, use_global_device_ids=true, to_apply=%region_10.11 | all-reduce | flops 64 | bytes 512 | tf_op jit(solution)/shard_map/psum | solution.py:115
  119.2 17.2 %psum.15 = f32[2,32]{1,0:T(2,128)S(1)} all-reduce(f32[2,32]{1,0:T(2,128)S(1)} %reduce_sum.103), channel_id=1, replica_groups=mesh['img'=4,'patch'=8] {'patch'}, use_global_device_ids=true, to_apply=%region_13.14 | all-reduce | flops 64 | bytes 512 | tf_op jit(solution)/shard_map/psum | solution.py:117
  136.9 1.3 fusion.44
  138.3 1.0 constant_dynamic-update-slice_fusion.2
  139.9 1.0 constant_dynamic-update-slice_fusion
  141.0 6.4 %fusion.38 = bf16[2,1,128,640]{3,2,1,0:T(8,128)(2,1)} fusion(f32[2,128,640]{2,1,0:T(8,128)S(1)} %get-tuple-element.18, bf16[5760,640,1]{1,0,2:T(8,128)(2,1)} %bitcast.115, bf16[2,1,128,5760]{3,2,0,1:T(8,128)(2,1)S(1)} %slice_dynamic-update-slice_fusion, f32[2,640]{1,0:T(2,128)S(1)} %copy-done.9, f32[640]{0:T(1024)S(1)} %copy-done.10), kind=kOutput, calls=%fused_computation.37 | convolution fusion | flops 1888092160 | bytes 11312640 | tf_op jit(solution)/shard_map/dot_general | solution.py:135
  (58 shorter events, 4.4 us)
Async XLA Ops:
  6.5 91.9 %copy-start = (bf16[640,640]{1,0:T(8,128)(2,1)S(1)}, bf16[640,640]{1,0:T(8,128)(2,1)}, u32[]{:S(2)}) copy-start(bf16[640,640]{1,0:T(8,128)(2,1)} %param.18) | copy-start | bytes 2457604
  6.5 67.3 %all-gather.3.cloned.1.call-start = ((), (), s32[]{:S(2)}) async-start(), calls=%async_computation | async-start | bytes 2949120 | tf_op jit(solution)/shard_map/all_gather | solution.py:93
  10.9 126.0 %collective-permute-start.1 = (bf16[2,1,128,640]{3,2,0,1:T(8,128)(2,1)}, bf16[2,1,128,640]{3,2,0,1:T(8,128)(2,1)}, u32[]{:S(2)}, u32[]{:S(2)}) collective-permute-start(bf16[2,1,128,640]{3,2,0,1:T(8,128)(2,1)} %bitcast.116), channel_id=1, source_target_pairs={{1,0},{2,1},{3,2},{4,3},{5,4},{6,5},{7,6},{9,8},{10,9},{11,10},{12... | collective-permute-start | bytes 983048 | tf_op jit(solution)/shard_map/ppermute | solution.py:19
  12.2 124.7 %collective-permute-start = (bf16[2,1,128,640]{3,2,0,1:T(8,128)(2,1)}, bf16[2,1,128,640]{3,2,0,1:T(8,128)(2,1)}, u32[]{:S(2)}, u32[]{:S(2)}) collective-permute-start(bf16[2,1,128,640]{3,2,0,1:T(8,128)(2,1)} %bitcast.117), channel_id=1, source_target_pairs={{0,1},{1,2},{2,3},{3,4},{4,5},{5,6},{6,7},{8,9},{9,10},{10,11},{11... | collective-permute-start | bytes 983048 | tf_op jit(solution)/shard_map/ppermute | solution.py:16
  24.1 49.7 %copy-start.3 = (bf16[2,128,640]{1,2,0:T(8,128)(2,1)}, bf16[2,128,640]{1,2,0:T(8,128)(2,1)S(1)}, u32[]{:S(2)}) copy-start(bf16[2,128,640]{1,2,0:T(8,128)(2,1)S(1)} %copy.28) | copy-start | bytes 983044
  25.7 1.1 copy-start.1
  93.1 2.5 %copy-start.5 = (bf16[2,1024,640]{1,2,0:T(8,128)(2,1)S(1)}, bf16[2,1024,640]{1,2,0:T(8,128)(2,1)}, u32[]{:S(2)}) copy-start(bf16[2,1024,640]{1,2,0:T(8,128)(2,1)} %copy.34) | copy-start | bytes 7864324
  95.6 2.4 %copy-start.2 = (f32[2,10,128,128]{2,3,1,0:T(8,128)S(1)}, f32[2,10,128,128]{2,3,1,0:T(8,128)}, u32[]{:S(2)}) copy-start(f32[2,10,128,128]{2,3,1,0:T(8,128)} %copy-done.1) | copy-start | bytes 3932164
  95.6 2.4 %copy-start.6 = (bf16[2,128,640]{1,2,0:T(8,128)(2,1)S(1)}, bf16[2,128,640]{1,2,0:T(8,128)(2,1)}, u32[]{:S(2)}) copy-start(bf16[2,128,640]{1,2,0:T(8,128)(2,1)} %copy.30) | copy-start | bytes 983044
  98.0 1.0 copy-start.4
  98.1 38.6 %copy-start.7 = (f32[640]{0:T(1024)S(1)}, f32[640]{0:T(1024)}, u32[]{:S(2)}) copy-start(f32[640]{0:T(1024)} %param.20) | copy-start | bytes 7684
  98.1 38.6 %copy-start.8 = (f32[640]{0:T(1024)S(1)}, f32[640]{0:T(1024)}, u32[]{:S(2)}) copy-start(f32[640]{0:T(1024)} %param.19) | copy-start | bytes 7684
  138.3 2.7 %copy-start.9 = (f32[2,640]{1,0:T(2,128)S(1)}, f32[2,640]{1,0:T(2,128)}, u32[]{:S(2)}) copy-start(f32[2,640]{1,0:T(2,128)} %param.23) | copy-start | bytes 15364
  138.3 2.7 %copy-start.10 = (f32[640]{0:T(1024)S(1)}, f32[640]{0:T(1024)}, u32[]{:S(2)}) copy-start(f32[640]{0:T(1024)} %param.22) | copy-start | bytes 7684
Sparse Core Ops, SparseCore 0:
  11.0 62.8 all-gather.2
where the time goes:
time: 155 us; the launch traced here: 154 us
  waiting for transfers between devices  46.9 us (30%)
  blocking collectives  36.2 us (23%)
  matrix products  23 us (15%)
  local copies, waits for them, and re-layouts  15.4 us (10%)
  between operations  13.7 us (9%)
  other arithmetic  11.4 us (7%)
  starting transfers between devices  7.56 us (5%)
    all_gather x1, waiting for transfers between devices, shards(): block_rows = lax.all_gather(stale_in, 'patch', axis=1, tiled=True)  46.8 us
    psum x1, blocking collectives, shards(): group_mean = lax.psum(jnp.sum(grouped, axis=(1, 3)), 'patch') / cell_count  19 us
    psum x1, blocking collectives, shards(): lax.psum(jnp.sum(centred * centred, axis=(1, 3)), 'patch') / cell_count  17.2 us
    dot_general x1, matrix products, shards(): jnp.einsum('snc,cd->snd', block_rows, w_pair, preferred_element_type=jnp....  6.47 us
    dot_general x1, matrix products, shards(): jnp.dot(unfolded, conv_weight.reshape(9 * channels, channels), preferred_...  6.35 us
    ppermute x1, starting transfers between devices, extended(): lax.ppermute(lax.slice_in_dim(block, block.shape[dim] - width, None, axis...  6.26 us
    slice x2, local copies, waits for them, and re-layouts, shards(): pair_rows[..., :channels]  4.69 us
    slice x1, local copies, waits for them, and re-layouts, shards(): pair_rows[..., channels:]  4.54 us
  transfers between devices with their start and end apart: 3, of which 1 were waited for; matrix products, arithmetic and copies ran while one was open for 22% of the time, Pallas kernels for 0%

commit v1 on v0

--- a/solution.py
+++ b/solution.py
@@ -90,7 +90,7 @@
         fresh_qkv[..., 2 * channels :],
         no_block,
     )
-    block_rows = lax.all_gather(stale_in, "patch", axis=1, tiled=True)
+    block_rows = jnp.concatenate(lax.all_gather(stale_in, axis_name="patch"), 1)
     pair_rows = jnp.einsum(
         "snc,cd->snd", block_rows, w_pair, preferred_element_type=jnp.float32
     ).astype(jnp.bfloat16)

time: 155 us -> 155 us (level)
  local copies, waits for them, and re-layouts: 15.4 us -> 17.9 us
  matrix products: 23 us -> 21 us
    all_gather x0 -> x1, local copies, waits for them, and re-layouts: none -> 2.16 us  [shards(): block_rows = jnp.concatenate(lax.all_gather(stale_in, axis_name='patch'), 1)]
    dot_general x1, matrix products: 6.47 us -> 4.47 us  [shards(): jnp.einsum('snc,cd->snd', block_rows, w_pair, preferred_element_type=jnp....]
    unnamed x29 -> x31, local copies, waits for them, and re-layouts: 4.02 us -> 4.33 us
where the time goes in v1:
time: 155 us
  waiting for transfers between devices  46.9 us (30%)
  blocking collectives  36.4 us (23%)
  matrix products  21 us (14%)
  local copies, waits for them, and re-layouts  17.9 us (12%)
  between operations  13.7 us (9%)
  other arithmetic  11.4 us (7%)
  starting transfers between devices  7.56 us (5%)
    all_gather x1, waiting for transfers between devices, shards(): block_rows = jnp.concatenate(lax.all_gather(stale_in, axis_name='patch'), 1)  46.9 us
    psum x1, blocking collectives, shards(): group_mean = lax.psum(jnp.sum(grouped, axis=(1, 3)), 'patch') / cell_count  19 us
    psum x1, blocking collectives, shards(): lax.psum(jnp.sum(centred * centred, axis=(1, 3)), 'patch') / cell_count  17.4 us
    dot_general x1, matrix products, shards(): jnp.dot(unfolded, conv_weight.reshape(9 * channels, channels), preferred_...  6.36 us
    ppermute x1, starting transfers between devices, extended(): lax.ppermute(lax.slice_in_dim(block, block.shape[dim] - width, None, axis...  6.26 us
    slice x2, local copies, waits for them, and re-layouts, shards(): pair_rows[..., :channels]  4.69 us
    slice x1, local copies, waits for them, and re-layouts, shards(): pair_rows[..., channels:]  4.54 us
    dot_general x1, matrix products, shards(): jnp.einsum('snc,cd->snd', block_rows, w_pair, preferred_element_type=jnp....  4.47 us
  transfers between devices with their start and end apart: 3, of which 1 were waited for; matrix products, arithmetic and copies ran while one was open for 22% of the time, Pallas kernels for 0%

profile of v1, /device:TPU:0, one launch (start us, length us, event | category | flops | bytes accessed | tf_op | source)
XLA Modules:
  0.0 154.9 jit_solution(299765751489458605)
XLA Ops:
  6.5 1.2 convert_reduce_fusion.1
  7.7 1.2 fusion.53
  8.9 1.9 %fusion.59 = bf16[2,1,128,640]{3,2,1,0:T(8,128)(2,1)} fusion(bf16[2,1,128,640]{3,2,1,0:T(8,128)(2,1)} %param.13, f32[2,128]{1,0:T(2,128)S(1)} %add_rsqrt_fusion.1, f32[2,128]{1,0:T(2,128)S(1)} %broadcast_multiply_fusion.1, f32[640]{0:T(1024)} %param.16, f32[640]{0:T(1024)} %param.15), kind=kLoop, calls=%fused_computation.62 | loop fusion | flops 983040 | bytes 662528 | tf_op jit(solution)/shard_map/convert_element_type | solution.py:29
  10.9 1.3 collective-permute-start.1
  12.2 6.3 %collective-permute-start = (bf16[2,1,128,640]{3,2,0,1:T(8,128)(2,1)}, bf16[2,1,128,640]{3,2,0,1:T(8,128)(2,1)}, u32[]{:S(2)}, u32[]{:S(2)}) collective-permute-start(bf16[2,1,128,640]{3,2,0,1:T(8,128)(2,1)} %bitcast.123), channel_id=1, source_target_pairs={{0,1},{1,2},{2,3},{3,4},{4,5},{5,6},{6,7},{8,9},{9,10},{10,11},{11... | collective-permute-start | bytes 983048 | tf_op jit(solution)/shard_map/ppermute | solution.py:16
  18.5 1.1 convert_reduce_fusion
  19.6 1.2 fusion.49
  20.8 3.0 %convolution_convert_fusion.1 = bf16[2,128,1920]{2,1,0:T(8,128)(2,1)S(1)} fusion(bf16[640,1920]{1,0:T(8,128)(2,1)} %param.17, bf16[2,1,128,640]{3,2,1,0:T(8,128)(2,1)} %param.12, f32[640]{0:T(1024)} %param.16, f32[640]{0:T(1024)} %param.15, f32[2,128]{1,0:T(2,128)S(1)} %add_rsqrt_fusion.2, f32[2,128]{1,0:T(2,128)S(1)} %broadcast_multiply_fusion.2), kind=kOutput, calls=%fused_computation.12 | convolution fusion | flops 630620160 | bytes 3775488 | tf_op jit(solution)/shard_map/stc,cd->std/dot_general | solution.py:75
  25.7 1.1 copy-done.1
  27.0 46.9 %all-gather.3.cloned.1.call-done = bf16[16,1,128,640]{3,2,1,0:T(8,128)(2,1)} async-done(((bf16[2,1,128,640]{3,2,1,0:T(8,128)(2,1)}), bf16[16,1,128,640]{3,2,1,0:T(8,128)(2,1)}) %all-gather.3.cloned.1.call-update) | async-done | bytes 2621456 | tf_op jit(solution)/shard_map/all_gather | solution.py:93
  73.9 2.2 %copy.48 = bf16[8,2,128,640]{3,2,0,1:T(8,128)(2,1)S(1)} copy(bf16[8,2,128,640]{3,2,1,0:T(8,128)(2,1)} %bitcast.115) | data formatting | bytes 5242880 | tf_op jit(solution)/shard_map/all_gather | solution.py:93
  76.3 4.5 %convolution_convert_fusion = bf16[2,1024,1280]{2,1,0:T(8,128)(2,1)S(1)} fusion(bf16[2,1024,640]{2,1,0:T(8,128)(2,1)S(1)} %bitcast.117, bf16[640,1920]{1,0:T(8,128)(2,1)S(1)} %copy-done.9), kind=kOutput, calls=%fused_computation.5 | convolution fusion | flops 3358064640 | bytes 9502720 | tf_op jit(solution)/shard_map/snc,cd->snd/dot_general | solution.py:94
  80.8 2.0 %fusion.76 = (bf16[2,1024,640]{2,1,0:T(8,128)(2,1)S(1)}, bf16[2,1024,640]{2,1,0:T(8,128)(2,1)}) fusion(bf16[2,1024,1280]{2,1,0:T(8,128)(2,1)S(1)} %convolution_convert_fusion), kind=kLoop, calls=%fused_computation.98 | loop fusion | bytes 10485760 | tf_op jit(solution)/shard_map/slice | solution.py:100
  82.8 4.5 %copy.50 = bf16[2,1024,640]{1,2,0:T(8,128)(2,1)} copy(bf16[2,1024,640]{2,1,0:T(8,128)(2,1)} %get-tuple-element.8) | data formatting | bytes 5242880 | tf_op jit(solution)/shard_map/slice | solution.py:100
  87.3 2.7 %copy.49 = bf16[2,1024,640]{1,2,0:T(8,128)(2,1)} copy(bf16[2,1024,640]{2,1,0:T(8,128)(2,1)S(1)} %get-tuple-element.7) | data formatting | bytes 5242880 | tf_op jit(solution)/shard_map/slice | solution.py:100
  90.1 3.5 %fusion = (f32[2,10,128]{2,1,0:T(8,128)S(1)}, f32[2,10,128,1024]{3,2,1,0:T(8,128)S(1)}) fusion(pred[1024]{0:T(1024)(128)(4,1)S(1)} %fusion.72, bf16[2,128,10,64]{1,3,2,0:T(8,128)(2,1)} %bitcast.114, bf16[2,1024,10,64]{1,3,2,0:T(8,128)(2,1)} %bitcast.112), kind=kOutput, calls=%fused_computation.2 | convolution fusion | flops 343406080 | bytes 13446144 | tf_op jit(solution)/shard_map/sqhd,skhd->shqk/dot_general | solution.py:38
  93.6 2.5 %fusion.1 = f32[2,10,128]{2,1,0:T(8,128)S(1)} fusion(f32[2,10,128,1024]{3,2,1,0:T(8,128)S(1)} %get-tuple-element.16, f32[2,10,128]{2,1,0:T(8,128)S(1)} %max.18, pred[1024]{0:T(1024)(128)(4,1)S(1)} %fusion.72), kind=kLoop, calls=%fused_computation.3 | loop fusion | flops 10483200 | bytes 10507264 | tf_op jit(solution)/shard_map/reduce_sum | solution.py:45
  96.1 2.4 %fusion.12 = f32[2,128,10,64]{1,3,2,0:T(8,128)S(1)} fusion(bf16[2,1024,10,64]{1,3,2,0:T(8,128)(2,1)S(1)} %bitcast.116, f32[2,10,128,1024]{3,2,1,0:T(8,128)S(1)} %get-tuple-element.16, f32[2,10,128]{2,1,0:T(8,128)S(1)} %max.18, pred[1024]{0:T(1024)(128)(4,1)S(1)} %fusion.72), kind=kOutput, calls=%fused_computation.19 | convolution fusion | flops 346030080 | bytes 13773824 | tf_op jit(solution)/shard_map/shqk,skhd->shqd/dot_general | solution.py:46
  100.2 19.0 %psum.14 = f32[2,32]{1,0:T(2,128)S(1)} all-reduce(f32[2,32]{1,0:T(2,128)S(1)} %reduce_sum.100), channel_id=1, replica_groups=mesh['img'=4,'patch'=8] {'patch'}, use_global_device_ids=true, to_apply=%region_10.11 | all-reduce | flops 64 | bytes 512 | tf_op jit(solution)/shard_map/psum | solution.py:115
  119.6 17.4 %psum.15 = f32[2,32]{1,0:T(2,128)S(1)} all-reduce(f32[2,32]{1,0:T(2,128)S(1)} %reduce_sum.103), channel_id=1, replica_groups=mesh['img'=4,'patch'=8] {'patch'}, use_global_device_ids=true, to_apply=%region_13.14 | all-reduce | flops 64 | bytes 512 | tf_op jit(solution)/shard_map/psum | solution.py:117
  137.5 1.3 fusion.43
  139.0 1.0 constant_dynamic-update-slice_fusion.2
  140.6 1.0 constant_dynamic-update-slice_fusion
  141.7 6.4 %fusion.37 = bf16[2,1,128,640]{3,2,1,0:T(8,128)(2,1)} fusion(f32[2,128,640]{2,1,0:T(8,128)S(1)} %get-tuple-element.18, bf16[5760,640,1]{1,0,2:T(8,128)(2,1)} %bitcast.121, bf16[2,1,128,5760]{3,2,0,1:T(8,128)(2,1)S(1)} %slice_dynamic-update-slice_fusion, f32[2,640]{1,0:T(2,128)S(1)} %copy-done.10, f32[640]{0:T(1024)S(1)} %copy-done.11), kind=kOutput, calls=%fused_computation.36 | convolution fusion | flops 1888092160 | bytes 11312640 | tf_op jit(solution)/shard_map/dot_general | solution.py:135
  (61 shorter events, 5.6 us)
Async XLA Ops:
  6.5 92.4 %copy-start = (bf16[640,640]{1,0:T(8,128)(2,1)S(1)}, bf16[640,640]{1,0:T(8,128)(2,1)}, u32[]{:S(2)}) copy-start(bf16[640,640]{1,0:T(8,128)(2,1)} %param.18) | copy-start | bytes 2457604
  6.5 67.3 %all-gather.3.cloned.1.call-start = ((), (), s32[]{:S(2)}) async-start(), calls=%async_computation | async-start | bytes 2949120 | tf_op jit(solution)/shard_map/all_gather | solution.py:93
  10.9 126.6 %collective-permute-start.1 = (bf16[2,1,128,640]{3,2,0,1:T(8,128)(2,1)}, bf16[2,1,128,640]{3,2,0,1:T(8,128)(2,1)}, u32[]{:S(2)}, u32[]{:S(2)}) collective-permute-start(bf16[2,1,128,640]{3,2,0,1:T(8,128)(2,1)} %bitcast.122), channel_id=1, source_target_pairs={{1,0},{2,1},{3,2},{4,3},{5,4},{6,5},{7,6},{9,8},{10,9},{11,10},{12... | collective-permute-start | bytes 983048 | tf_op jit(solution)/shard_map/ppermute | solution.py:19
  12.2 125.3 %collective-permute-start = (bf16[2,1,128,640]{3,2,0,1:T(8,128)(2,1)}, bf16[2,1,128,640]{3,2,0,1:T(8,128)(2,1)}, u32[]{:S(2)}, u32[]{:S(2)}) collective-permute-start(bf16[2,1,128,640]{3,2,0,1:T(8,128)(2,1)} %bitcast.123), channel_id=1, source_target_pairs={{0,1},{1,2},{2,3},{3,4},{4,5},{5,6},{6,7},{8,9},{9,10},{10,11},{11... | collective-permute-start | bytes 983048 | tf_op jit(solution)/shard_map/ppermute | solution.py:16
  24.1 51.9 %copy-start.3 = (bf16[2,128,640]{1,2,0:T(8,128)(2,1)}, bf16[2,128,640]{1,2,0:T(8,128)(2,1)S(1)}, u32[]{:S(2)}) copy-start(bf16[2,128,640]{1,2,0:T(8,128)(2,1)S(1)} %copy.42) | copy-start | bytes 983044
  25.7 1.1 copy-start.1
  73.9 2.5 %copy-start.9 = (bf16[640,1920]{1,0:T(8,128)(2,1)S(1)}, bf16[640,1920]{1,0:T(8,128)(2,1)}, u32[]{:S(2)}) copy-start(bf16[640,1920]{1,0:T(8,128)(2,1)} %param.17) | copy-start | bytes 7372804
  93.6 2.5 %copy-start.5 = (bf16[2,1024,640]{1,2,0:T(8,128)(2,1)S(1)}, bf16[2,1024,640]{1,2,0:T(8,128)(2,1)}, u32[]{:S(2)}) copy-start(bf16[2,1024,640]{1,2,0:T(8,128)(2,1)} %copy.50) | copy-start | bytes 7864324
  96.1 2.4 %copy-start.2 = (f32[2,10,128,128]{2,3,1,0:T(8,128)S(1)}, f32[2,10,128,128]{2,3,1,0:T(8,128)}, u32[]{:S(2)}) copy-start(f32[2,10,128,128]{2,3,1,0:T(8,128)} %copy-done.1) | copy-start | bytes 3932164
  96.1 2.4 %copy-start.6 = (bf16[2,128,640]{1,2,0:T(8,128)(2,1)S(1)}, bf16[2,128,640]{1,2,0:T(8,128)(2,1)}, u32[]{:S(2)}) copy-start(bf16[2,128,640]{1,2,0:T(8,128)(2,1)} %copy.44) | copy-start | bytes 983044
  98.5 1.0 copy-start.4
  98.5 38.8 %copy-start.7 = (f32[640]{0:T(1024)S(1)}, f32[640]{0:T(1024)}, u32[]{:S(2)}) copy-start(f32[640]{0:T(1024)} %param.20) | copy-start | bytes 7684
  98.5 38.7 %copy-start.8 = (f32[640]{0:T(1024)S(1)}, f32[640]{0:T(1024)}, u32[]{:S(2)}) copy-start(f32[640]{0:T(1024)} %param.19) | copy-start | bytes 7684
  138.9 2.7 %copy-start.10 = (f32[2,640]{1,0:T(2,128)S(1)}, f32[2,640]{1,0:T(2,128)}, u32[]{:S(2)}) copy-start(f32[2,640]{1,0:T(2,128)} %param.23) | copy-start | bytes 15364
  138.9 2.7 %copy-start.11 = (f32[640]{0:T(1024)S(1)}, f32[640]{0:T(1024)}, u32[]{:S(2)}) copy-start(f32[640]{0:T(1024)} %param.22) | copy-start | bytes 7684
Sparse Core Ops, SparseCore 0:
  11.0 62.8 all-gather.2
